TPU v7x, 512 devices: a whole 4x8x8 slice. The times are simulated.
512 devices in a mesh: row: 16 (over y, core), col: 32 (over z, x).
Axes of the slice: x: 4, y: 8, z: 8, core: 2. Of those that a mesh axis runs over, the one named last changes fastest.
Arguments:
- matrix: float32 [16384, 16384], P('row', 'col'), as said below
Outputs:
- hess_panel: float32 [16384, 8], P('row')
- reflectors: float32 [16384, 8], P('row')
- wy_products: float32 [16384, 8], P('row')
- wy_factor: float32 [8, 8], replicated
Inputs may be any that keep to these rules, and one draw needn't show every extreme that they name: Entries matrix[i+1, i] lie within 2.5 +- 6 / sqrt(16384); every other entry within +- 6 / sqrt(16384).
All inputs are finite; a program needn't handle non-finite values.
Results may differ from a plain program's by a relative error of at most 0.0003.
Values sent between devices are 32-bit elements; how exact they have to be, the bound alone decides.
A program may use at most 128 MiB of HBM per device.

v0:
```python
import functools

import jax
import jax.numpy as jnp
from jax import lax
from jax.experimental import pallas as pl
from jax.experimental.pallas import tpu as pltpu
from jax.sharding import PartitionSpec as P

NB = 8
LANES = 128
SUB = 8
STATS = 16
BLOCK = 256
F32 = jnp.float32
BF16 = jnp.bfloat16


def kernel(
    nrow, ncol, a_hbm, hess_ref, refl_ref, wy_ref, fac_ref,
    a_ref, first_ref, pan_ref, mypan_ref, part_ref, got_ref, stat_ref, stats_ref,
    vec_ref, yvec_ref,
    load_sem, first_sem, pan0_send, pan0_sem, pan_send, pan_sem, stat_send, stat_sem,
    part_send, part_sem, v_send, v_sem, y_send, y_sem,
):
    rows_local, cols_local = a_hbm.shape
    tiles = cols_local // LANES
    lines = rows_local // LANES
    split = rows_local // cols_local
    row, col = lax.axis_index("row"), lax.axis_index("col")
    blocks = rows_local // BLOCK

    def wrap(value, bound):
        return jnp.where(value >= bound, value - bound, value)

    def peers_of_row(dr, act, skip):
        to_row = wrap(row + dr, nrow)
        for dc in range(1 if skip else 0, ncol):
            act(to_row, wrap(col + dc, ncol))

    def block_load(i):
        span = pl.ds(i * BLOCK, BLOCK)
        return pltpu.make_async_copy(a_hbm.at[span], a_ref.at[span], load_sem.at[i])

    head = pltpu.make_async_copy(a_hbm.at[:, pl.ds(0, LANES)], first_ref, first_sem)

    @pl.when(col == 0)
    def _():
        head.start()

    for i in range(blocks):
        block_load(i).start(priority=1)

    barrier = pltpu.get_barrier_semaphore()

    def greet(to_row, to_col):
        pl.semaphore_signal(
            barrier, inc=1, device_id=(to_row, to_col),
            device_id_type=pl.DeviceIdType.MESH,
        )

    def greet_row(dr, carry):
        peers_of_row(dr, greet, False)
        return carry

    lax.fori_loop(1, nrow, greet_row, 0)
    peers_of_row(0, greet, True)

    def send(src, dst, send_sem, recv_sem, to_row, to_col):
        pltpu.make_async_remote_copy(
            src_ref=src, dst_ref=dst, send_sem=send_sem, recv_sem=recv_sem,
            device_id=(to_row, to_col), device_id_type=pl.DeviceIdType.MESH,
        ).start()

    def place(src, dst, send_sem, recv_sem, to_row, to_col, here):
        @pl.when(here)
        def _():
            pltpu.make_async_copy(src, dst, recv_sem).start()

        @pl.when(jnp.logical_not(here))
        def _():
            send(src, dst, send_sem, recv_sem, to_row, to_col)

    def expect(ref, sem):
        pltpu.make_async_copy(ref, ref, sem).wait()

    def settle(ref, sem, here):
        count = ref.shape[1]

        @pl.when(jnp.logical_not(here))
        def _():
            expect(ref, sem)

        if count > 1:
            @pl.when(here)
            def _():
                expect(ref.at[:, pl.ds(0, count - 1)], sem)

    def spread(piece_of, dst, send_sem, recv_sem):
        for h in range(split):
            to_col = row * split + h
            for dr in range(nrow - 1, 0, -1):
                send(piece_of(h), dst, send_sem, recv_sem, wrap(row + dr, nrow), to_col)
            place(piece_of(h), dst, send_sem, recv_sem, row, to_col, to_col == col)

    @pl.when(col == 0)
    def _():
        head.wait()
        for h in range(split):
            def turn(t, carry):
                at = pl.multiple_of(h * cols_local + t * LANES, LANES)
                block = first_ref[pl.ds(at, LANES), :].T
                for k in range(NB + 1):
                    pan_ref[k, h, pl.ds(t, 1), :] = block[k : k + 1, :]
                return carry

            lax.fori_loop(0, tiles, turn, 0)

    pl.semaphore_wait(barrier, nrow * ncol - 1)

    @pl.when(col == 0)
    def _():
        spread(
            lambda h: pan_ref.at[pl.ds(0, 1), h], mypan_ref.at[pl.ds(0, 1)],
            pan0_send, pan0_sem,
        )
        spread(
            lambda h: pan_ref.at[pl.ds(1, NB), h], mypan_ref.at[pl.ds(1, NB)],
            pan_send, pan_sem,
        )

    ones = jnp.ones((SUB, 2 * LANES), BF16)

    def fold(acc, t, j):
        high = acc.astype(BF16)
        low = (acc - high.astype(F32)).astype(BF16)
        both = jnp.concatenate([high, low], axis=1)
        res = lax.dot_general(
            ones, both, (((1,), (1,)), ((), ())), preferred_element_type=F32
        )
        h = t // tiles
        part_ref[j, h, pl.ds(t - h * tiles, 1), :] = res[0:1, :]

    def matvec(j, vector):
        pieces = [
            jnp.broadcast_to(vector[t : t + 1, :], (SUB, LANES)) for t in range(tiles)
        ]

        def product(t):
            accs = []
            for s in range(LANES // SUB):
                at = pl.ds(pl.multiple_of(t * LANES + s * SUB, SUB), SUB)
                acc = a_ref[at, pl.ds(0, LANES)] * pieces[0]
                for p in range(1, tiles):
                    acc = acc + a_ref[at, pl.ds(p * LANES, LANES)] * pieces[p]
                accs.append(acc)
            return jnp.concatenate(accs, axis=0)

        per = BLOCK // LANES
        if j == 0:
            def loaded(i, carry):
                block_load(i).wait()
                for k in range(per):
                    fold(product(i * per + k), i * per + k, j)
                return carry

            lax.fori_loop(0, blocks, loaded, 0)
        else:
            def step(t, acc):
                fold(acc, t - 1, j)
                return product(t)

            fold(lax.fori_loop(1, lines, step, product(0)), lines - 1, j)

    owner = col // split
    slot = col - owner * split
    home = jnp.logical_and(owner == row, lax.rem(col, nrow) == row)

    def publish(src, ref, j, send_sem, recv_sem):
        for i in range(split):
            to_col = row + nrow * i
            here = jnp.logical_and(owner == row, to_col == col)
            place(src, ref.at[j, slot], send_sem, recv_sem, owner, to_col, here)

    lane = lax.broadcasted_iota(jnp.int32, (1, LANES), 1)
    line_ids = lax.broadcasted_iota(jnp.int32, (tiles, LANES), 0) * LANES
    ids = line_ids + lax.broadcasted_iota(jnp.int32, (tiles, LANES), 1)
    ids = ids + col * cols_local
    hess_ref[...] = jnp.zeros_like(hess_ref)

    factor = [[None] * NB for _ in range(NB)]
    gram = [[None] * NB for _ in range(NB)]
    tops = []
    images = []
    expect(mypan_ref.at[pl.ds(0, 1)], pan0_sem)
    b = mypan_ref[0]
    for j in range(NB):
        rows = [jnp.sum(vec_ref[k] * b, axis=0, keepdims=True) for k in range(j)]
        rows += [jnp.zeros((1, LANES), F32)] * (NB - j)
        rows.append(jnp.sum(b * b, axis=0, keepdims=True))
        rows.append(jnp.where(col == 0, b[0:1, :], F32(0.0)))
        rows += [jnp.zeros((1, LANES), F32)] * (STATS - NB - 2)
        stat = jnp.concatenate(rows, axis=0)
        stat_ref[j] = stat
        stats_ref[j, pl.ds(col, 1)] = stat[None]
        peers_of_row(
            0,
            lambda to_row, to_col: send(
                stat_ref.at[j], stats_ref.at[j, col], stat_send, stat_sem.at[j],
                to_row, to_col,
            ),
            True,
        )
        if j > 0:
            publish(vec_ref.at[j - 1], refl_ref, j - 1, v_send, v_sem)
            publish(yvec_ref.at[j - 1], wy_ref, j - 1, y_send, y_sem)
        matvec(j, b)
        spread(lambda h: part_ref.at[j, h], got_ref.at[j, col], part_send, part_sem.at[j])

        expect(stats_ref.at[j, pl.ds(0, ncol - 1)], stat_sem.at[j])
        stat = stats_ref[j, 0]
        for i in range(1, ncol):
            stat = stat + stats_ref[j, i]
        sums = jnp.sum(stat, axis=1, keepdims=True)
        inner = [sums[k : k + 1, :] for k in range(j)]
        top = stat[NB + 1 : NB + 2, :]
        weight = []
        for m in range(j):
            value = factor[0][m] * inner[0]
            for k in range(1, m + 1):
                value = value + factor[k][m] * inner[k]
            weight.append(value)
        for m in range(j):
            top = top - tops[m] * weight[m]
        above = jnp.where(lane <= j, top, F32(0.0))
        square = sums[NB : NB + 1, :] - jnp.sum(above * above, axis=1, keepdims=True)
        norm = jnp.sqrt(square)
        alpha = top[:, j + 1 : j + 2]
        signed = jnp.where(alpha >= 0, norm, -norm)
        scale = 1.0 / jnp.sqrt(norm * (norm + jnp.abs(alpha)))
        u = b
        for m in range(j):
            u = u - vec_ref[m] * weight[m]
        u = jnp.where(ids > j, u, F32(0.0)) + jnp.where(ids == j + 1, signed, F32(0.0))
        u = u * scale
        vec_ref[j] = u
        vtop = jnp.where(lane > j, top, F32(0.0))
        vtop = (vtop + jnp.where(lane == j + 1, signed, F32(0.0))) * scale
        couple = []
        for k in range(j):
            value = inner[k]
            for m in range(j):
                value = value - gram[k][m] * weight[m]
            fix = jnp.where(lane == j + 1, signed, F32(0.0)) - above
            value = value + jnp.sum(tops[k] * fix, axis=1, keepdims=True)
            couple.append(value * scale)
        for k in range(j):
            value = factor[k][k] * couple[k]
            for m in range(k + 1, j):
                value = value + factor[k][m] * couple[m]
            factor[k][j] = -value
            gram[k][j] = couple[k]
            gram[j][k] = couple[k]
        factor[j][j] = jnp.ones((1, 1), F32)
        gram[j][j] = jnp.full((1, 1), 2.0, F32)
        tops.append(vtop)
        hrow = jnp.where(lane == j + 1, -signed, above)
        hess_ref[j, 0, 0:1, :] = jnp.where(row == 0, hrow, F32(0.0))
        if j == 0:
            expect(mypan_ref.at[pl.ds(1, NB)], pan_sem)
        drop = jnp.zeros((tiles, LANES), F32)
        for k in range(j):
            drop = drop + images[k] * weight[k]
        for i in range(j + 1):
            drop = drop + mypan_ref[i] * top[:, i : i + 1]
        drop = drop - mypan_ref[j + 1] * signed
        back = jnp.zeros((tiles, LANES), F32)
        for k in range(j):
            back = back + yvec_ref[k] * couple[k]
        if j + 1 < NB:
            rest = mypan_ref[j + 1]
            for k in range(j):
                rest = rest - yvec_ref[k] * tops[k][:, j + 1 : j + 2]

        expect(got_ref.at[j], part_sem.at[j])
        image = got_ref[j, 0]
        for i in range(1, ncol):
            image = image + got_ref[j, i]
        image = (image - drop) * scale
        images.append(image)
        if j + 1 == NB:
            publish(vec_ref.at[j], refl_ref, j, v_send, v_sem)
        new_y = image - back
        yvec_ref[j] = new_y
        if j + 1 < NB:
            b = rest - new_y * vtop[:, j + 1 : j + 2]

    publish(yvec_ref.at[NB - 1], wy_ref, NB - 1, y_send, y_sem)
    at_row = lax.broadcasted_iota(jnp.int32, (NB, NB), 0)
    at_col = lax.broadcasted_iota(jnp.int32, (NB, NB), 1)
    fac = jnp.zeros((NB, NB), F32)
    for k in range(NB):
        for m in range(k, NB):
            here = jnp.logical_and(at_row == k, at_col == m)
            fac = jnp.where(here, jnp.broadcast_to(factor[k][m], (NB, NB)), fac)
    fac_ref[...] = fac

    expect(refl_ref, v_sem)
    expect(wy_ref, y_sem)
    settle(got_ref, part_send, owner == row)
    settle(refl_ref, v_send, home)
    settle(wy_ref, y_send, home)
    expect(stats_ref.at[:, pl.ds(0, ncol - 1)], stat_send)

    @pl.when(col == 0)
    def _():
        settle(got_ref.at[pl.ds(0, 1)], pan0_send, row == 0)
        settle(got_ref, pan_send, row == 0)


def finish(hess_in, refl_in, wy_in, fac_in, hess_out, refl_out, wy_out, fac_out):
    split, tiles = hess_in.shape[1:3]
    for src, dst in ((hess_in, hess_out), (refl_in, refl_out), (wy_in, wy_out)):
        for h in range(split):
            for t in range(tiles):
                span = pl.ds((h * tiles + t) * LANES, LANES)
                for k in range(NB):
                    dst[k : k + 1, span] = src[k, h, t : t + 1, :]
    fac_out[...] = fac_in[...]


def shards(nrow, ncol, matrix):
    rows_local, cols_local = matrix.shape
    tiles = cols_local // LANES
    split = rows_local // cols_local
    blocks = rows_local // BLOCK
    panel = jax.ShapeDtypeStruct((NB, split, tiles, LANES), F32)
    vmem = pl.BlockSpec(memory_space=pltpu.VMEM)
    dma = pltpu.SemaphoreType.DMA
    hess, refl, wy, fac = pl.pallas_call(
        functools.partial(kernel, nrow, ncol),
        out_shape=(panel, panel, panel, jax.ShapeDtypeStruct((NB, NB), F32)),
        in_specs=[pl.BlockSpec(memory_space=pl.ANY)],
        out_specs=(vmem, vmem, vmem, vmem),
        scratch_shapes=[
            pltpu.VMEM((rows_local, cols_local), F32),
            pltpu.VMEM((rows_local, LANES), F32),
            pltpu.VMEM((NB + 1, split, tiles, LANES), F32),
            pltpu.VMEM((NB + 1, tiles, LANES), F32),
            pltpu.VMEM((NB, split, tiles, LANES), F32),
            pltpu.VMEM((NB, ncol, tiles, LANES), F32),
            pltpu.VMEM((NB, STATS, LANES), F32),
            pltpu.VMEM((NB, ncol, STATS, LANES), F32),
            pltpu.VMEM((NB, tiles, LANES), F32),
            pltpu.VMEM((NB, tiles, LANES), F32),
            dma((blocks,)),
            dma(()),
            dma(()),
            dma(()),
            dma(()),
            dma(()),
            dma(()),
            dma((NB,)),
            dma(()),
            dma((NB,)),
            dma(()),
            dma(()),
            dma(()),
            dma(()),
        ],
        compiler_params=pltpu.CompilerParams(
            collective_id=0, has_side_effects=True, vmem_limit_bytes=56 * 2**20
        ),
    )(matrix)

    flat = jax.ShapeDtypeStruct((NB, rows_local), F32)
    hess, refl, wy, fac = pl.pallas_call(
        finish,
        out_shape=(flat, flat, flat, jax.ShapeDtypeStruct((NB, NB), F32)),
        in_specs=[vmem] * 4,
        out_specs=(vmem,) * 4,
    )(hess, refl, wy, fac)
    return hess.T, refl.T, wy.T, fac


def solution(mesh):
    nrow, ncol = mesh.shape["row"], mesh.shape["col"]
    return jax.shard_map(
        functools.partial(shards, nrow, ncol),
        mesh=mesh,
        in_specs=(P("row", "col"),),
        out_specs=(P("row", None), P("row", None), P("row", None), P()),
        check_vma=False,
    )
```

profile of v0, /device:TPU:1, one launch (start us, length us, event | category | flops | bytes accessed | tf_op | source)
XLA Modules:
  0.0 130.3 jit_solution(10835454336488164693)
XLA Ops:
  0.6 128.2 %shard_map.46 = (f32[8,2,4,128]{3,2,1,0:T(4,128)}, f32[8,2,4,128]{3,2,1,0:T(4,128)}, f32[8,2,4,128]{3,2,1,0:T(4,128)}, f32[8,8]{1,0:T(8,128)}) custom-call(f32[1024,512]{1,0:T(8,128)} %a_hbm.1), custom_call_target="tpu_custom_call" | custom-call | tf_op jit(solution)/shard_map/pallas_call | solution.py:340
  128.8 1.5 %shard_map.47 = (f32[8,1024]{1,0:T(8,128)}, f32[8,1024]{1,0:T(8,128)}, f32[8,1024]{1,0:T(8,128)}, f32[8,8]{1,0:T(8,128)}) custom-call(f32[8,2,4,128]{3,2,1,0:T(4,128)} %get-tuple-element.12.hess_in, f32[8,2,4,128]{3,2,1,0:T(4,128)} %get-tuple-element.13.refl_in, f32[8,2,4,128]{3,2,1,0:T(4,128)} %get-tuple-element.14.wy_in, f32[8,8]{1,0:T(8,128)} %get-tuple-element.15.fac_in), custom_call_target="tpu_custom_call" | custom-call | tf_op jit(solution)/shard_map/pallas_call | solution.py:377
where the time goes:
time: 131 us; the launch traced here: 130 us
  Pallas kernels  130 us (99%)
    pallas_call x1, Pallas kernels, shards(): pl.pallas_call(functools.partial(kernel, nrow, ncol), out_shape=(panel, p...  128 us

commit v1 on v0

--- a/solution.py
+++ b/solution.py
@@ -20,7 +20,7 @@
     nrow, ncol, a_hbm, hess_ref, refl_ref, wy_ref, fac_ref,
     a_ref, first_ref, pan_ref, mypan_ref, part_ref, got_ref, stat_ref, stats_ref,
     vec_ref, yvec_ref,
-    load_sem, first_sem, pan0_send, pan0_sem, pan_send, pan_sem, stat_send, stat_sem,
+    load_sem, first_sem, pan_send, pan_sem, stat_send, stat_sem,
     part_send, part_sem, v_send, v_sem, y_send, y_sem,
 ):
     rows_local, cols_local = a_hbm.shape
@@ -29,14 +29,16 @@
     split = rows_local // cols_local
     row, col = lax.axis_index("row"), lax.axis_index("col")
     blocks = rows_local // BLOCK
+    owner = col // split
+    slot = col - owner * split
+    home = owner == row
+    last = NB - 1
 
     def wrap(value, bound):
         return jnp.where(value >= bound, value - bound, value)
 
-    def peers_of_row(dr, act, skip):
-        to_row = wrap(row + dr, nrow)
-        for dc in range(1 if skip else 0, ncol):
-            act(to_row, wrap(col + dc, ncol))
+    def far_first(count):
+        return sorted(range(count), key=lambda d: -min(d, count - d))
 
     def block_load(i):
         span = pl.ds(i * BLOCK, BLOCK)
@@ -59,12 +61,15 @@
             device_id_type=pl.DeviceIdType.MESH,
         )
 
-    def greet_row(dr, carry):
-        peers_of_row(dr, greet, False)
-        return carry
-
-    lax.fori_loop(1, nrow, greet_row, 0)
-    peers_of_row(0, greet, True)
+    for dc in far_first(ncol)[:-1]:
+        greet(owner, wrap(col + dc, ncol))
+
+    @pl.when(jnp.logical_not(home))
+    def _():
+        greet(owner, col)
+
+    for dc in far_first(ncol)[:-1]:
+        greet(row, wrap(col + dc, ncol))
 
     def send(src, dst, send_sem, recv_sem, to_row, to_col):
         pltpu.make_async_remote_copy(
@@ -81,6 +86,10 @@
         def _():
             send(src, dst, send_sem, recv_sem, to_row, to_col)
 
+    def to_peers(src, dst, send_sem, recv_sem):
+        for dc in far_first(ncol)[:-1]:
+            send(src, dst, send_sem, recv_sem, row, wrap(col + dc, ncol))
+
     def expect(ref, sem):
         pltpu.make_async_copy(ref, ref, sem).wait()
 
@@ -96,12 +105,11 @@
             def _():
                 expect(ref.at[:, pl.ds(0, count - 1)], sem)
 
-    def spread(piece_of, dst, send_sem, recv_sem):
-        for h in range(split):
-            to_col = row * split + h
-            for dr in range(nrow - 1, 0, -1):
-                send(piece_of(h), dst, send_sem, recv_sem, wrap(row + dr, nrow), to_col)
-            place(piece_of(h), dst, send_sem, recv_sem, row, to_col, to_col == col)
+    def spread(h, src, dst, send_sem, recv_sem):
+        to_col = row * split + h
+        for dr in far_first(nrow)[:-1]:
+            send(src, dst, send_sem, recv_sem, wrap(row + dr, nrow), to_col)
+        place(src, dst, send_sem, recv_sem, row, to_col, to_col == col)
 
     @pl.when(col == 0)
     def _():
@@ -116,32 +124,36 @@
 
             lax.fori_loop(0, tiles, turn, 0)
 
-    pl.semaphore_wait(barrier, nrow * ncol - 1)
-
-    @pl.when(col == 0)
-    def _():
-        spread(
-            lambda h: pan_ref.at[pl.ds(0, 1), h], mypan_ref.at[pl.ds(0, 1)],
-            pan0_send, pan0_sem,
-        )
-        spread(
-            lambda h: pan_ref.at[pl.ds(1, NB), h], mypan_ref.at[pl.ds(1, NB)],
-            pan_send, pan_sem,
-        )
+    partners = split * nrow + ncol - 1
+    pl.semaphore_wait(barrier, jnp.where(home, partners - 1, partners))
+
+    def pan_span(i):
+        return pl.ds(0, 1) if i == 0 else pl.ds(2 * i - 1, 2)
+
+    def send_pan(i):
+        @pl.when(col == 0)
+        def _():
+            for h in range(split):
+                spread(
+                    h, pan_ref.at[pan_span(i), h], mypan_ref.at[pan_span(i)],
+                    pan_send, pan_sem.at[i],
+                )
+
+    send_pan(0)
+    send_pan(1)
 
     ones = jnp.ones((SUB, 2 * LANES), BF16)
 
-    def fold(acc, t, j):
+    def fold(acc, h, t, j):
         high = acc.astype(BF16)
         low = (acc - high.astype(F32)).astype(BF16)
         both = jnp.concatenate([high, low], axis=1)
         res = lax.dot_general(
             ones, both, (((1,), (1,)), ((), ())), preferred_element_type=F32
         )
-        h = t // tiles
-        part_ref[j, h, pl.ds(t - h * tiles, 1), :] = res[0:1, :]
-
-    def matvec(j, vector):
+        part_ref[j, h, pl.ds(t, 1), :] = res[0:1, :]
+
+    def matvec(j, vector, act):
         pieces = [
             jnp.broadcast_to(vector[t : t + 1, :], (SUB, LANES)) for t in range(tiles)
         ]
@@ -156,74 +168,84 @@
                 accs.append(acc)
             return jnp.concatenate(accs, axis=0)
 
-        per = BLOCK // LANES
-        if j == 0:
-            def loaded(i, carry):
-                block_load(i).wait()
-                for k in range(per):
-                    fold(product(i * per + k), i * per + k, j)
-                return carry
-
-            lax.fori_loop(0, blocks, loaded, 0)
-        else:
+        for h in range(split):
             def step(t, acc):
-                fold(acc, t - 1, j)
-                return product(t)
-
-            fold(lax.fori_loop(1, lines, step, product(0)), lines - 1, j)
-
-    owner = col // split
-    slot = col - owner * split
-    home = jnp.logical_and(owner == row, lax.rem(col, nrow) == row)
+                fold(acc, h, t - 1, j)
+                return product(h * tiles + t)
+
+            fold(lax.fori_loop(1, tiles, step, product(h * tiles)), h, tiles - 1, j)
+            act(h)
 
     def publish(src, ref, j, send_sem, recv_sem):
         for i in range(split):
-            to_col = row + nrow * i
-            here = jnp.logical_and(owner == row, to_col == col)
+            to_col = row * split + i
+            here = jnp.logical_and(home, to_col == col)
             place(src, ref.at[j, slot], send_sem, recv_sem, owner, to_col, here)
 
     lane = lax.broadcasted_iota(jnp.int32, (1, LANES), 1)
+    at_stat = lax.broadcasted_iota(jnp.int32, (STATS, LANES), 0) + STATS
+    at_lane = lax.broadcasted_iota(jnp.int32, (STATS, LANES), 1)
     line_ids = lax.broadcasted_iota(jnp.int32, (tiles, LANES), 0) * LANES
     ids = line_ids + lax.broadcasted_iota(jnp.int32, (tiles, LANES), 1)
     ids = ids + col * cols_local
     hess_ref[...] = jnp.zeros_like(hess_ref)
 
+    def send_stats(j, b):
+        rows = [jnp.sum(vec_ref[k] * b, axis=0, keepdims=True) for k in range(j)]
+        rows += [jnp.zeros((1, LANES), F32)] * (NB - j)
+        rows.append(jnp.sum(b * b, axis=0, keepdims=True))
+        rows += [jnp.zeros((1, LANES), F32)] * (STATS - NB - 1)
+        sums = jnp.sum(jnp.concatenate(rows, axis=0), axis=1, keepdims=True)
+        packed = jnp.where(at_lane == at_stat, sums, F32(0.0))
+        packed = jnp.sum(packed, axis=0, keepdims=True)
+        top = jnp.where(jnp.logical_and(col == 0, lane < STATS), b[0:1, :], packed)
+        stat_ref[j] = top
+        stats_ref[j, col] = top
+        to_peers(stat_ref.at[j], stats_ref.at[j, col], stat_send, stat_sem.at[j])
+
+    def total(ref, j, count):
+        terms = [ref[j, i] for i in range(count)]
+        while len(terms) > 1:
+            terms = [x + y for x, y in zip(terms[::2], terms[1::2])]
+        return terms[0]
+
     factor = [[None] * NB for _ in range(NB)]
     gram = [[None] * NB for _ in range(NB)]
     tops = []
     images = []
-    expect(mypan_ref.at[pl.ds(0, 1)], pan0_sem)
+    for i in range(blocks):
+        block_load(i).wait()
+    expect(mypan_ref.at[pan_span(0)], pan_sem.at[0])
     b = mypan_ref[0]
     for j in range(NB):
-        rows = [jnp.sum(vec_ref[k] * b, axis=0, keepdims=True) for k in range(j)]
-        rows += [jnp.zeros((1, LANES), F32)] * (NB - j)
-        rows.append(jnp.sum(b * b, axis=0, keepdims=True))
-        rows.append(jnp.where(col == 0, b[0:1, :], F32(0.0)))
-        rows += [jnp.zeros((1, LANES), F32)] * (STATS - NB - 2)
-        stat = jnp.concatenate(rows, axis=0)
-        stat_ref[j] = stat
-        stats_ref[j, pl.ds(col, 1)] = stat[None]
-        peers_of_row(
-            0,
-            lambda to_row, to_col: send(
-                stat_ref.at[j], stats_ref.at[j, col], stat_send, stat_sem.at[j],
-                to_row, to_col,
-            ),
-            True,
-        )
-        if j > 0:
+        if j < last:
+            matvec(j, b, lambda h: spread(
+                h, part_ref.at[j, h], got_ref.at[j, col], part_send, part_sem.at[j]
+            ))
+            send_stats(j, b)
+            if j > 0:
+                publish(vec_ref.at[j - 1], refl_ref, j - 1, v_send, v_sem)
+                publish(yvec_ref.at[j - 1], wy_ref, j - 1, y_send, y_sem)
+            if 0 < j < NB // 2:
+                send_pan(j + 1)
+        else:
+            send_stats(j, b)
+
+            def to_owner(h):
+                to_col = row * split + h
+                place(
+                    part_ref.at[j, h], got_ref.at[j, col], part_send, part_sem.at[j],
+                    row, to_col, to_col == col,
+                )
+
+            matvec(j, b, to_owner)
             publish(vec_ref.at[j - 1], refl_ref, j - 1, v_send, v_sem)
             publish(yvec_ref.at[j - 1], wy_ref, j - 1, y_send, y_sem)
-        matvec(j, b)
-        spread(lambda h: part_ref.at[j, h], got_ref.at[j, col], part_send, part_sem.at[j])
 
         expect(stats_ref.at[j, pl.ds(0, ncol - 1)], stat_sem.at[j])
-        stat = stats_ref[j, 0]
-        for i in range(1, ncol):
-            stat = stat + stats_ref[j, i]
-        sums = jnp.sum(stat, axis=1, keepdims=True)
-        inner = [sums[k : k + 1, :] for k in range(j)]
-        top = stat[NB + 1 : NB + 2, :]
+        stat = total(stats_ref, j, ncol)
+        inner = [stat[:, STATS + k : STATS + k + 1] for k in range(j)]
+        top = jnp.where(lane < STATS, stat, F32(0.0))
         weight = []
         for m in range(j):
             value = factor[0][m] * inner[0]
@@ -233,7 +255,8 @@
         for m in range(j):
             top = top - tops[m] * weight[m]
         above = jnp.where(lane <= j, top, F32(0.0))
-        square = sums[NB : NB + 1, :] - jnp.sum(above * above, axis=1, keepdims=True)
+        square = stat[:, STATS + NB : STATS + NB + 1]
+        square = square - jnp.sum(above * above, axis=1, keepdims=True)
         norm = jnp.sqrt(square)
         alpha = top[:, j + 1 : j + 2]
         signed = jnp.where(alpha >= 0, norm, -norm)
@@ -244,6 +267,11 @@
         u = jnp.where(ids > j, u, F32(0.0)) + jnp.where(ids == j + 1, signed, F32(0.0))
         u = u * scale
         vec_ref[j] = u
+        if j == last:
+            @pl.when(home)
+            def _():
+                to_peers(vec_ref.at[j], refl_ref.at[j, slot], v_send, v_sem)
+                pltpu.make_async_copy(vec_ref.at[j], refl_ref.at[j, slot], v_sem).start()
         vtop = jnp.where(lane > j, top, F32(0.0))
         vtop = (vtop + jnp.where(lane == j + 1, signed, F32(0.0))) * scale
         couple = []
@@ -266,36 +294,40 @@
         tops.append(vtop)
         hrow = jnp.where(lane == j + 1, -signed, above)
         hess_ref[j, 0, 0:1, :] = jnp.where(row == 0, hrow, F32(0.0))
-        if j == 0:
-            expect(mypan_ref.at[pl.ds(1, NB)], pan_sem)
+        if j % 2 == 0:
+            expect(mypan_ref.at[pan_span(j // 2 + 1)], pan_sem.at[j // 2 + 1])
         drop = jnp.zeros((tiles, LANES), F32)
         for k in range(j):
             drop = drop + images[k] * weight[k]
         for i in range(j + 1):
             drop = drop + mypan_ref[i] * top[:, i : i + 1]
-        drop = drop - mypan_ref[j + 1] * signed
+        drop = (drop - mypan_ref[j + 1] * signed) * scale
         back = jnp.zeros((tiles, LANES), F32)
         for k in range(j):
             back = back + yvec_ref[k] * couple[k]
-        if j + 1 < NB:
+        if j < last:
             rest = mypan_ref[j + 1]
             for k in range(j):
                 rest = rest - yvec_ref[k] * tops[k][:, j + 1 : j + 2]
-
-        expect(got_ref.at[j], part_sem.at[j])
-        image = got_ref[j, 0]
-        for i in range(1, ncol):
-            image = image + got_ref[j, i]
-        image = (image - drop) * scale
-        images.append(image)
-        if j + 1 == NB:
-            publish(vec_ref.at[j], refl_ref, j, v_send, v_sem)
-        new_y = image - back
-        yvec_ref[j] = new_y
-        if j + 1 < NB:
-            b = rest - new_y * vtop[:, j + 1 : j + 2]
-
-    publish(yvec_ref.at[NB - 1], wy_ref, NB - 1, y_send, y_sem)
+            pull = vtop[:, j + 1 : j + 2]
+            rest = rest + (drop + back) * pull
+            pull = pull * scale
+
+            expect(got_ref.at[j], part_sem.at[j])
+            image = total(got_ref, j, ncol)
+            b = rest - image * pull
+            image = image * scale - drop
+            images.append(image)
+            yvec_ref[j] = image - back
+        else:
+            @pl.when(home)
+            def _():
+                expect(got_ref.at[j], part_sem.at[j])
+                image = total(got_ref, j, ncol)
+                yvec_ref[j] = image * scale - drop - back
+                to_peers(yvec_ref.at[j], wy_ref.at[j, slot], y_send, y_sem)
+                pltpu.make_async_copy(yvec_ref.at[j], wy_ref.at[j, slot], y_sem).start()
+
     at_row = lax.broadcasted_iota(jnp.int32, (NB, NB), 0)
     at_col = lax.broadcasted_iota(jnp.int32, (NB, NB), 1)
     fac = jnp.zeros((NB, NB), F32)
@@ -305,17 +337,24 @@
             fac = jnp.where(here, jnp.broadcast_to(factor[k][m], (NB, NB)), fac)
     fac_ref[...] = fac
 
+    expect(stats_ref.at[:, pl.ds(0, ncol - 1)], stat_send)
+    settle(got_ref.at[pl.ds(0, last)], part_send, home)
+    settle(got_ref.at[pl.ds(0, 1), pl.ds(0, split)], part_send, home)
+    settle(refl_ref.at[pl.ds(0, last)], v_send, home)
+    settle(wy_ref.at[pl.ds(0, last)], y_send, home)
+
+    @pl.when(home)
+    def _():
+        expect(got_ref.at[0, pl.ds(0, ncol - 1)], v_send)
+        expect(got_ref.at[0, pl.ds(0, ncol - 1)], y_send)
+
+    @pl.when(col == 0)
+    def _():
+        settle(got_ref.at[pl.ds(0, 1)], pan_send, row == 0)
+        settle(got_ref, pan_send, row == 0)
+
     expect(refl_ref, v_sem)
     expect(wy_ref, y_sem)
-    settle(got_ref, part_send, owner == row)
-    settle(refl_ref, v_send, home)
-    settle(wy_ref, y_send, home)
-    expect(stats_ref.at[:, pl.ds(0, ncol - 1)], stat_send)
-
-    @pl.when(col == 0)
-    def _():
-        settle(got_ref.at[pl.ds(0, 1)], pan0_send, row == 0)
-        settle(got_ref, pan_send, row == 0)
 
 
 def finish(hess_in, refl_in, wy_in, fac_in, hess_out, refl_out, wy_out, fac_out):
@@ -349,16 +388,14 @@
             pltpu.VMEM((NB + 1, tiles, LANES), F32),
             pltpu.VMEM((NB, split, tiles, LANES), F32),
             pltpu.VMEM((NB, ncol, tiles, LANES), F32),
-            pltpu.VMEM((NB, STATS, LANES), F32),
-            pltpu.VMEM((NB, ncol, STATS, LANES), F32),
+            pltpu.VMEM((NB, 1, LANES), F32),
+            pltpu.VMEM((NB, ncol, 1, LANES), F32),
             pltpu.VMEM((NB, tiles, LANES), F32),
             pltpu.VMEM((NB, tiles, LANES), F32),
             dma((blocks,)),
             dma(()),
             dma(()),
-            dma(()),
-            dma(()),
-            dma(()),
+            dma((NB // 2 + 1,)),
             dma(()),
             dma((NB,)),
             dma(()),

time: 131 us -> 100 us (0.76)
  Pallas kernels: 130 us -> 98.4 us
    pallas_call x1, Pallas kernels: 128 us -> 96.9 us  [shards(): pl.pallas_call(functools.partial(kernel, nrow, ncol), out_shape=(panel, p...]
where the time goes in v1:
time: 100 us; the launch traced here: 99.1 us
  Pallas kernels  98.4 us (98%)
    pallas_call x1, Pallas kernels, shards(): pl.pallas_call(functools.partial(kernel, nrow, ncol), out_shape=(panel, p...  96.9 us

profile of v1, /device:TPU:1, one launch (start us, length us, event | category | flops | bytes accessed | tf_op | source)
XLA Modules:
  0.0 99.1 jit_solution(3252744389484967493)
XLA Ops:
  0.6 96.9 %shard_map.46 = (f32[8,2,4,128]{3,2,1,0:T(4,128)}, f32[8,2,4,128]{3,2,1,0:T(4,128)}, f32[8,2,4,128]{3,2,1,0:T(4,128)}, f32[8,8]{1,0:T(8,128)}) custom-call(f32[1024,512]{1,0:T(8,128)} %a_hbm.1), custom_call_target="tpu_custom_call" | custom-call | tf_op jit(solution)/shard_map/pallas_call | solution.py:379
  97.6 1.5 %shard_map.47 = (f32[8,1024]{1,0:T(8,128)}, f32[8,1024]{1,0:T(8,128)}, f32[8,1024]{1,0:T(8,128)}, f32[8,8]{1,0:T(8,128)}) custom-call(f32[8,2,4,128]{3,2,1,0:T(4,128)} %get-tuple-element.12.hess_in, f32[8,2,4,128]{3,2,1,0:T(4,128)} %get-tuple-element.13.refl_in, f32[8,2,4,128]{3,2,1,0:T(4,128)} %get-tuple-element.14.wy_in, f32[8,8]{1,0:T(8,128)} %get-tuple-element.15.fac_in), custom_call_target="tpu_custom_call" | custom-call | tf_op jit(solution)/shard_map/pallas_call | solution.py:414

commit v2 on v1

--- a/solution.py
+++ b/solution.py
@@ -19,9 +19,10 @@
 def kernel(
     nrow, ncol, a_hbm, hess_ref, refl_ref, wy_ref, fac_ref,
     a_ref, first_ref, pan_ref, mypan_ref, part_ref, got_ref, stat_ref, stats_ref,
-    vec_ref, yvec_ref,
+    vec_ref, yvec_ref, edges_ref, tail_ref, ends_ref, sums_ref,
     load_sem, first_sem, pan_send, pan_sem, stat_send, stat_sem,
     part_send, part_sem, v_send, v_sem, y_send, y_sem,
+    edge_send, edge_sem, tail_send, tail_sem, sum_send, sum_sem,
 ):
     rows_local, cols_local = a_hbm.shape
     tiles = cols_local // LANES
@@ -175,6 +176,12 @@
 
             fold(lax.fori_loop(1, tiles, step, product(h * tiles)), h, tiles - 1, j)
             act(h)
+
+    def own_rows(src, dst, send_sem, recv_sem):
+        @pl.when(home)
+        def _():
+            to_peers(src, dst(slot), send_sem, recv_sem)
+            pltpu.make_async_copy(src, dst(slot), recv_sem).start()
 
     def publish(src, ref, j, send_sem, recv_sem):
         for i in range(split):
@@ -203,8 +210,8 @@
         stats_ref[j, col] = top
         to_peers(stat_ref.at[j], stats_ref.at[j, col], stat_send, stat_sem.at[j])
 
-    def total(ref, j, count):
-        terms = [ref[j, i] for i in range(count)]
+    def total(ref, count):
+        terms = [ref[i] for i in range(count)]
         while len(terms) > 1:
             terms = [x + y for x, y in zip(terms[::2], terms[1::2])]
         return terms[0]
@@ -224,26 +231,20 @@
             ))
             send_stats(j, b)
             if j > 0:
-                publish(vec_ref.at[j - 1], refl_ref, j - 1, v_send, v_sem)
                 publish(yvec_ref.at[j - 1], wy_ref, j - 1, y_send, y_sem)
             if 0 < j < NB // 2:
                 send_pan(j + 1)
         else:
             send_stats(j, b)
-
-            def to_owner(h):
-                to_col = row * split + h
-                place(
-                    part_ref.at[j, h], got_ref.at[j, col], part_send, part_sem.at[j],
-                    row, to_col, to_col == col,
-                )
-
-            matvec(j, b, to_owner)
-            publish(vec_ref.at[j - 1], refl_ref, j - 1, v_send, v_sem)
-            publish(yvec_ref.at[j - 1], wy_ref, j - 1, y_send, y_sem)
+            tail_ref[0] = b
+            tail_ref[1] = yvec_ref[j - 1]
+            matvec(j, b, lambda h: None)
+            sums_ref[col] = part_ref[j]
+            to_peers(part_ref.at[j], sums_ref.at[col], sum_send, sum_sem)
+            own_rows(tail_ref, lambda at: ends_ref.at[at], tail_send, tail_sem)
 
         expect(stats_ref.at[j, pl.ds(0, ncol - 1)], stat_sem.at[j])
-        stat = total(stats_ref, j, ncol)
+        stat = total(stats_ref.at[j], ncol)
         inner = [stat[:, STATS + k : STATS + k + 1] for k in range(j)]
         top = jnp.where(lane < STATS, stat, F32(0.0))
         weight = []
@@ -267,11 +268,8 @@
         u = jnp.where(ids > j, u, F32(0.0)) + jnp.where(ids == j + 1, signed, F32(0.0))
         u = u * scale
         vec_ref[j] = u
-        if j == last:
-            @pl.when(home)
-            def _():
-                to_peers(vec_ref.at[j], refl_ref.at[j, slot], v_send, v_sem)
-                pltpu.make_async_copy(vec_ref.at[j], refl_ref.at[j, slot], v_sem).start()
+        if j < last:
+            publish(vec_ref.at[j], refl_ref, j, v_send, v_sem)
         vtop = jnp.where(lane > j, top, F32(0.0))
         vtop = (vtop + jnp.where(lane == j + 1, signed, F32(0.0))) * scale
         couple = []
@@ -294,39 +292,67 @@
         tops.append(vtop)
         hrow = jnp.where(lane == j + 1, -signed, above)
         hess_ref[j, 0, 0:1, :] = jnp.where(row == 0, hrow, F32(0.0))
-        if j % 2 == 0:
-            expect(mypan_ref.at[pan_span(j // 2 + 1)], pan_sem.at[j // 2 + 1])
-        drop = jnp.zeros((tiles, LANES), F32)
-        for k in range(j):
-            drop = drop + images[k] * weight[k]
-        for i in range(j + 1):
-            drop = drop + mypan_ref[i] * top[:, i : i + 1]
-        drop = (drop - mypan_ref[j + 1] * signed) * scale
-        back = jnp.zeros((tiles, LANES), F32)
-        for k in range(j):
-            back = back + yvec_ref[k] * couple[k]
+        if j == 0 or 1 < j <= NB // 2:
+            i = max(j, 1)
+            expect(mypan_ref.at[pan_span(i)], pan_sem.at[i])
         if j < last:
+            drop = jnp.zeros((tiles, LANES), F32)
+            for k in range(j):
+                drop = drop + images[k] * weight[k]
+            for i in range(j + 1):
+                drop = drop + mypan_ref[i] * top[:, i : i + 1]
+            drop = (drop - mypan_ref[j + 1] * signed) * scale
+            back = jnp.zeros((tiles, LANES), F32)
+            for k in range(j):
+                back = back + yvec_ref[k] * couple[k]
             rest = mypan_ref[j + 1]
             for k in range(j):
                 rest = rest - yvec_ref[k] * tops[k][:, j + 1 : j + 2]
             pull = vtop[:, j + 1 : j + 2]
             rest = rest + (drop + back) * pull
             pull = pull * scale
+            if 0 < j <= NB // 2 + 1:
+                own_rows(
+                    mypan_ref.at[pan_span(j - 1)],
+                    lambda at: edges_ref.at[at, pan_span(j - 1)],
+                    edge_send, edge_sem,
+                )
 
             expect(got_ref.at[j], part_sem.at[j])
-            image = total(got_ref, j, ncol)
+            image = total(got_ref.at[j], ncol)
             b = rest - image * pull
             image = image * scale - drop
             images.append(image)
             yvec_ref[j] = image - back
-        else:
-            @pl.when(home)
-            def _():
-                expect(got_ref.at[j], part_sem.at[j])
-                image = total(got_ref, j, ncol)
-                yvec_ref[j] = image * scale - drop - back
-                to_peers(yvec_ref.at[j], wy_ref.at[j, slot], y_send, y_sem)
-                pltpu.make_async_copy(yvec_ref.at[j], wy_ref.at[j, slot], y_sem).start()
+
+    mix = []
+    for m in range(last):
+        value = weight[m]
+        for k in range(m + 1, last):
+            value = value + gram[m][k] * weight[k]
+        mix.append(value * scale + couple[m])
+    expect(edges_ref, edge_sem)
+    expect(wy_ref.at[pl.ds(0, last - 1)], y_sem)
+    rest = []
+    for h in range(split):
+        value = edges_ref[h, NB] * signed
+        for i in range(NB):
+            value = value - edges_ref[h, i] * top[:, i : i + 1]
+        value = value * scale
+        for k in range(last - 1):
+            value = value - wy_ref[k, h] * mix[k]
+        rest.append(value)
+    expect(refl_ref.at[pl.ds(0, last)], v_sem)
+    expect(ends_ref, tail_sem)
+    for h in range(split):
+        at = line_ids + lane + (row * rows_local + h * cols_local)
+        u = ends_ref[h, 0]
+        for m in range(last):
+            u = u - refl_ref[m, h] * weight[m]
+        u = jnp.where(at > last, u, F32(0.0)) + jnp.where(at == NB, signed, F32(0.0))
+        refl_ref[last, h] = u * scale
+        wy_ref[last - 1, h] = ends_ref[h, 1]
+        rest[h] = rest[h] - ends_ref[h, 1] * mix[last - 1]
 
     at_row = lax.broadcasted_iota(jnp.int32, (NB, NB), 0)
     at_col = lax.broadcasted_iota(jnp.int32, (NB, NB), 1)
@@ -339,22 +365,27 @@
 
     expect(stats_ref.at[:, pl.ds(0, ncol - 1)], stat_send)
     settle(got_ref.at[pl.ds(0, last)], part_send, home)
-    settle(got_ref.at[pl.ds(0, 1), pl.ds(0, split)], part_send, home)
     settle(refl_ref.at[pl.ds(0, last)], v_send, home)
-    settle(wy_ref.at[pl.ds(0, last)], y_send, home)
+    settle(wy_ref.at[pl.ds(0, last - 1)], y_send, home)
 
     @pl.when(home)
     def _():
-        expect(got_ref.at[0, pl.ds(0, ncol - 1)], v_send)
-        expect(got_ref.at[0, pl.ds(0, ncol - 1)], y_send)
+        expect(got_ref.at[pl.ds(0, NB + 1), pl.ds(0, ncol - 1)], edge_send)
 
     @pl.when(col == 0)
     def _():
-        settle(got_ref.at[pl.ds(0, 1)], pan_send, row == 0)
-        settle(got_ref, pan_send, row == 0)
-
-    expect(refl_ref, v_sem)
-    expect(wy_ref, y_sem)
+        settle(got_ref.at[pl.ds(0, NB + 1)], pan_send, row == 0)
+
+    others = sums_ref.at[pl.ds(0, ncol - 1)]
+    expect(others, sum_sem)
+    image = total(sums_ref, ncol)
+    for h in range(split):
+        wy_ref[last, h] = image[h] * scale + rest[h]
+    expect(others, sum_send)
+
+    @pl.when(home)
+    def _():
+        expect(others, tail_send)
 
 
 def finish(hess_in, refl_in, wy_in, fac_in, hess_out, refl_out, wy_out, fac_out):
@@ -387,11 +418,15 @@
             pltpu.VMEM((NB + 1, split, tiles, LANES), F32),
             pltpu.VMEM((NB + 1, tiles, LANES), F32),
             pltpu.VMEM((NB, split, tiles, LANES), F32),
-            pltpu.VMEM((NB, ncol, tiles, LANES), F32),
+            pltpu.VMEM((NB + 1, ncol, tiles, LANES), F32),
             pltpu.VMEM((NB, 1, LANES), F32),
             pltpu.VMEM((NB, ncol, 1, LANES), F32),
             pltpu.VMEM((NB, tiles, LANES), F32),
             pltpu.VMEM((NB, tiles, LANES), F32),
+            pltpu.VMEM((split, NB + 1, tiles, LANES), F32),
+            pltpu.VMEM((2, tiles, LANES), F32),
+            pltpu.VMEM((split, 2, tiles, LANES), F32),
+            pltpu.VMEM((ncol, split, tiles, LANES), F32),
             dma((blocks,)),
             dma(()),
             dma(()),
@@ -400,6 +435,12 @@
             dma((NB,)),
             dma(()),
             dma((NB,)),
+            dma(()),
+            dma(()),
+            dma(()),
+            dma(()),
+            dma(()),
+            dma(()),
             dma(()),
             dma(()),
             dma(()),

time: 100 us -> 97.4 us (0.974)
  Pallas kernels: 98.4 us -> 96.6 us
    pallas_call x1, Pallas kernels: 96.9 us -> 95.1 us  [shards(): pl.pallas_call(functools.partial(kernel, nrow, ncol), out_shape=(panel, p...]
where the time goes in v2:
time: 97.4 us; the launch traced here: 97.2 us
  Pallas kernels  96.6 us (99%)
    pallas_call x1, Pallas kernels, shards(): pl.pallas_call(functools.partial(kernel, nrow, ncol), out_shape=(panel, p...  95.1 us

profile of v2, /device:TPU:1, one launch (start us, length us, event | category | flops | bytes accessed | tf_op | source)
XLA Modules:
  0.0 97.2 jit_solution(7309784883339878010)
XLA Ops:
  0.6 95.1 %shard_map.46 = (f32[8,2,4,128]{3,2,1,0:T(4,128)}, f32[8,2,4,128]{3,2,1,0:T(4,128)}, f32[8,2,4,128]{3,2,1,0:T(4,128)}, f32[8,8]{1,0:T(8,128)}) custom-call(f32[1024,512]{1,0:T(8,128)} %a_hbm.1), custom_call_target="tpu_custom_call" | custom-call | tf_op jit(solution)/shard_map/pallas_call | solution.py:410
  95.7 1.5 %shard_map.47 = (f32[8,1024]{1,0:T(8,128)}, f32[8,1024]{1,0:T(8,128)}, f32[8,1024]{1,0:T(8,128)}, f32[8,8]{1,0:T(8,128)}) custom-call(f32[8,2,4,128]{3,2,1,0:T(4,128)} %get-tuple-element.12.hess_in, f32[8,2,4,128]{3,2,1,0:T(4,128)} %get-tuple-element.13.refl_in, f32[8,2,4,128]{3,2,1,0:T(4,128)} %get-tuple-element.14.wy_in, f32[8,8]{1,0:T(8,128)} %get-tuple-element.15.fac_in), custom_call_target="tpu_custom_call" | custom-call | tf_op jit(solution)/shard_map/pallas_call | solution.py:455

commit v3 on v2

--- a/solution.py
+++ b/solution.py
@@ -13,20 +13,18 @@
 STATS = 16
 BLOCK = 256
 F32 = jnp.float32
-BF16 = jnp.bfloat16
 
 
 def kernel(
-    nrow, ncol, a_hbm, hess_ref, refl_ref, wy_ref, fac_ref,
-    a_ref, first_ref, pan_ref, mypan_ref, part_ref, got_ref, stat_ref, stats_ref,
-    vec_ref, yvec_ref, edges_ref, tail_ref, ends_ref, sums_ref,
+    nrow, ncol, a_hbm, hess_out, refl_out, wy_out, fac_ref,
+    refl_ref, wy_ref, a_ref, first_ref, pan_ref, mypan_ref, part_ref, got_ref, stat_ref, stats_ref,
+    vec_ref, yvec_ref, edges_ref, tail_ref, ends_ref, sums_ref, coef_ref,
     load_sem, first_sem, pan_send, pan_sem, stat_send, stat_sem,
     part_send, part_sem, v_send, v_sem, y_send, y_sem,
     edge_send, edge_sem, tail_send, tail_sem, sum_send, sum_sem,
 ):
     rows_local, cols_local = a_hbm.shape
     tiles = cols_local // LANES
-    lines = rows_local // LANES
     split = rows_local // cols_local
     row, col = lax.axis_index("row"), lax.axis_index("col")
     blocks = rows_local // BLOCK
@@ -106,10 +104,12 @@
             def _():
                 expect(ref.at[:, pl.ds(0, count - 1)], sem)
 
-    def spread(h, src, dst, send_sem, recv_sem):
+    def spread_out(h, src, dst, send_sem, recv_sem):
+        for dr in far_first(nrow)[:-1]:
+            send(src, dst, send_sem, recv_sem, wrap(row + dr, nrow), row * split + h)
+
+    def spread_here(h, src, dst, send_sem, recv_sem):
         to_col = row * split + h
-        for dr in far_first(nrow)[:-1]:
-            send(src, dst, send_sem, recv_sem, wrap(row + dr, nrow), to_col)
         place(src, dst, send_sem, recv_sem, row, to_col, to_col == col)
 
     @pl.when(col == 0)
@@ -134,25 +134,18 @@
     def send_pan(i):
         @pl.when(col == 0)
         def _():
-            for h in range(split):
-                spread(
-                    h, pan_ref.at[pan_span(i), h], mypan_ref.at[pan_span(i)],
-                    pan_send, pan_sem.at[i],
-                )
+            for spread in (spread_out, spread_here):
+                for h in range(split):
+                    spread(
+                        h, pan_ref.at[pan_span(i), h], mypan_ref.at[pan_span(i)],
+                        pan_send, pan_sem.at[i],
+                    )
 
     send_pan(0)
     send_pan(1)
 
-    ones = jnp.ones((SUB, 2 * LANES), BF16)
-
     def fold(acc, h, t, j):
-        high = acc.astype(BF16)
-        low = (acc - high.astype(F32)).astype(BF16)
-        both = jnp.concatenate([high, low], axis=1)
-        res = lax.dot_general(
-            ones, both, (((1,), (1,)), ((), ())), preferred_element_type=F32
-        )
-        part_ref[j, h, pl.ds(t, 1), :] = res[0:1, :]
+        part_ref[j, h, t : t + 1, :] = jnp.sum(acc.T, axis=0, keepdims=True)
 
     def matvec(j, vector, act):
         pieces = [
@@ -162,7 +155,7 @@
         def product(t):
             accs = []
             for s in range(LANES // SUB):
-                at = pl.ds(pl.multiple_of(t * LANES + s * SUB, SUB), SUB)
+                at = pl.ds(t * LANES + s * SUB, SUB)
                 acc = a_ref[at, pl.ds(0, LANES)] * pieces[0]
                 for p in range(1, tiles):
                     acc = acc + a_ref[at, pl.ds(p * LANES, LANES)] * pieces[p]
@@ -170,11 +163,8 @@
             return jnp.concatenate(accs, axis=0)
 
         for h in range(split):
-            def step(t, acc):
-                fold(acc, h, t - 1, j)
-                return product(h * tiles + t)
-
-            fold(lax.fori_loop(1, tiles, step, product(h * tiles)), h, tiles - 1, j)
+            for t in range(tiles):
+                fold(product(h * tiles + t), h, t, j)
             act(h)
 
     def own_rows(src, dst, send_sem, recv_sem):
@@ -182,6 +172,12 @@
         def _():
             to_peers(src, dst(slot), send_sem, recv_sem)
             pltpu.make_async_copy(src, dst(slot), recv_sem).start()
+
+    def lay_out(ref, out, k):
+        for h in range(split):
+            for t in range(tiles):
+                span = pl.ds((h * tiles + t) * LANES, LANES)
+                out[k : k + 1, span] = ref[k, h, t : t + 1, :]
 
     def publish(src, ref, j, send_sem, recv_sem):
         for i in range(split):
@@ -195,7 +191,7 @@
     line_ids = lax.broadcasted_iota(jnp.int32, (tiles, LANES), 0) * LANES
     ids = line_ids + lax.broadcasted_iota(jnp.int32, (tiles, LANES), 1)
     ids = ids + col * cols_local
-    hess_ref[...] = jnp.zeros_like(hess_ref)
+    hess_out[...] = jnp.zeros_like(hess_out)
 
     def send_stats(j, b):
         rows = [jnp.sum(vec_ref[k] * b, axis=0, keepdims=True) for k in range(j)]
@@ -226,9 +222,14 @@
     b = mypan_ref[0]
     for j in range(NB):
         if j < last:
-            matvec(j, b, lambda h: spread(
-                h, part_ref.at[j, h], got_ref.at[j, col], part_send, part_sem.at[j]
-            ))
+            def share(spread, h):
+                spread(
+                    h, part_ref.at[j, h], got_ref.at[j, col], part_send, part_sem.at[j]
+                )
+
+            matvec(j, b, functools.partial(share, spread_out))
+            for h in range(split):
+                share(spread_here, h)
             send_stats(j, b)
             if j > 0:
                 publish(yvec_ref.at[j - 1], wy_ref, j - 1, y_send, y_sem)
@@ -291,7 +292,7 @@
         gram[j][j] = jnp.full((1, 1), 2.0, F32)
         tops.append(vtop)
         hrow = jnp.where(lane == j + 1, -signed, above)
-        hess_ref[j, 0, 0:1, :] = jnp.where(row == 0, hrow, F32(0.0))
+        hess_out[j : j + 1, 0:LANES] = jnp.where(row == 0, hrow, F32(0.0))
         if j == 0 or 1 < j <= NB // 2:
             i = max(j, 1)
             expect(mypan_ref.at[pan_span(i)], pan_sem.at[i])
@@ -310,7 +311,9 @@
                 rest = rest - yvec_ref[k] * tops[k][:, j + 1 : j + 2]
             pull = vtop[:, j + 1 : j + 2]
             rest = rest + (drop + back) * pull
-            pull = pull * scale
+            coef_ref[0] = jnp.broadcast_to(pull * scale, (tiles, LANES))
+            coef_ref[1] = jnp.broadcast_to(scale, (tiles, LANES))
+            coef_ref[2] = rest
             if 0 < j <= NB // 2 + 1:
                 own_rows(
                     mypan_ref.at[pan_span(j - 1)],
@@ -320,8 +323,8 @@
 
             expect(got_ref.at[j], part_sem.at[j])
             image = total(got_ref.at[j], ncol)
-            b = rest - image * pull
-            image = image * scale - drop
+            b = coef_ref[2] - image * coef_ref[0]
+            image = image * coef_ref[1] - drop
             images.append(image)
             yvec_ref[j] = image - back
 
@@ -376,11 +379,16 @@
     def _():
         settle(got_ref.at[pl.ds(0, NB + 1)], pan_send, row == 0)
 
+    for k in range(NB):
+        lay_out(refl_ref, refl_out, k)
+    for k in range(last):
+        lay_out(wy_ref, wy_out, k)
     others = sums_ref.at[pl.ds(0, ncol - 1)]
     expect(others, sum_sem)
     image = total(sums_ref, ncol)
     for h in range(split):
         wy_ref[last, h] = image[h] * scale + rest[h]
+    lay_out(wy_ref, wy_out, last)
     expect(others, sum_send)
 
     @pl.when(home)
@@ -388,15 +396,16 @@
         expect(others, tail_send)
 
 
-def finish(hess_in, refl_in, wy_in, fac_in, hess_out, refl_out, wy_out, fac_out):
-    split, tiles = hess_in.shape[1:3]
-    for src, dst in ((hess_in, hess_out), (refl_in, refl_out), (wy_in, wy_out)):
-        for h in range(split):
-            for t in range(tiles):
-                span = pl.ds((h * tiles + t) * LANES, LANES)
-                for k in range(NB):
-                    dst[k : k + 1, span] = src[k, h, t : t + 1, :]
-    fac_out[...] = fac_in[...]
+def finish(*refs):
+    count = len(refs) // 2
+    sems = refs[-1]
+    copies = [
+        pltpu.make_async_copy(refs[i], refs[count + i], sems.at[i]) for i in range(count)
+    ]
+    for copy in copies:
+        copy.start()
+    for copy in copies:
+        copy.wait()
 
 
 def shards(nrow, ncol, matrix):
@@ -404,15 +413,17 @@
     tiles = cols_local // LANES
     split = rows_local // cols_local
     blocks = rows_local // BLOCK
-    panel = jax.ShapeDtypeStruct((NB, split, tiles, LANES), F32)
+    panel = pltpu.VMEM((NB, rows_local), F32)
     vmem = pl.BlockSpec(memory_space=pltpu.VMEM)
     dma = pltpu.SemaphoreType.DMA
     hess, refl, wy, fac = pl.pallas_call(
         functools.partial(kernel, nrow, ncol),
-        out_shape=(panel, panel, panel, jax.ShapeDtypeStruct((NB, NB), F32)),
+        out_shape=(panel, panel, panel, pltpu.VMEM((NB, NB), F32)),
         in_specs=[pl.BlockSpec(memory_space=pl.ANY)],
         out_specs=(vmem, vmem, vmem, vmem),
         scratch_shapes=[
+            pltpu.VMEM((NB, split, tiles, LANES), F32),
+            pltpu.VMEM((NB, split, tiles, LANES), F32),
             pltpu.VMEM((rows_local, cols_local), F32),
             pltpu.VMEM((rows_local, LANES), F32),
             pltpu.VMEM((NB + 1, split, tiles, LANES), F32),
@@ -427,6 +438,7 @@
             pltpu.VMEM((2, tiles, LANES), F32),
             pltpu.VMEM((split, 2, tiles, LANES), F32),
             pltpu.VMEM((ncol, split, tiles, LANES), F32),
+            pltpu.VMEM((3, tiles, LANES), F32),
             dma((blocks,)),
             dma(()),
             dma(()),
@@ -450,14 +462,16 @@
             collective_id=0, has_side_effects=True, vmem_limit_bytes=56 * 2**20
         ),
     )(matrix)
-
-    flat = jax.ShapeDtypeStruct((NB, rows_local), F32)
+    made = [
+        pltpu.with_memory_space_constraint(x, pltpu.VMEM) for x in (hess, refl, wy, fac)
+    ]
     hess, refl, wy, fac = pl.pallas_call(
         finish,
-        out_shape=(flat, flat, flat, jax.ShapeDtypeStruct((NB, NB), F32)),
+        out_shape=[jax.ShapeDtypeStruct(x.shape, F32) for x in made],
         in_specs=[vmem] * 4,
-        out_specs=(vmem,) * 4,
-    )(hess, refl, wy, fac)
+        out_specs=[pl.BlockSpec(memory_space=pl.ANY)] * 4,
+        scratch_shapes=[dma((4,))],
+    )(*made)
     return hess.T, refl.T, wy.T, fac
 
 

time: 97.4 us -> 89.2 us (0.916)
  Pallas kernels: 96.6 us -> 88.2 us
    pallas_call x1, Pallas kernels: 95.1 us -> 87.5 us  [shards(): pl.pallas_call(functools.partial(kernel, nrow, ncol), out_shape=(panel, p...]
where the time goes in v3:
time: 89.2 us; the launch traced here: 88.8 us
  Pallas kernels  88.2 us (99%)
    pallas_call x1, Pallas kernels, shards(): pl.pallas_call(functools.partial(kernel, nrow, ncol), out_shape=(panel, p...  87.5 us

profile of v3, /device:TPU:1, one launch (start us, length us, event | category | flops | bytes accessed | tf_op | source)
XLA Modules:
  0.0 88.8 jit_solution(3646178842785114108)
XLA Ops:
  0.6 87.5 %shard_map.46 = (f32[8,1024]{1,0:T(8,128)S(1)}, f32[8,1024]{1,0:T(8,128)S(1)}, f32[8,1024]{1,0:T(8,128)S(1)}, f32[8,8]{1,0:T(8,128)S(1)}) custom-call(f32[1024,512]{1,0:T(8,128)} %a_hbm.1), custom_call_target="tpu_custom_call" | custom-call | tf_op jit(solution)/shard_map/pallas_call | solution.py:419
  88.1 0.7 shard_map.47

commit v4 on v3

--- a/solution.py
+++ b/solution.py
@@ -12,16 +12,19 @@
 SUB = 8
 STATS = 16
 BLOCK = 256
+CORES = 2
+CHIPS_X = 4
 F32 = jnp.float32
 
 
 def kernel(
     nrow, ncol, a_hbm, hess_out, refl_out, wy_out, fac_ref,
     refl_ref, wy_ref, a_ref, first_ref, pan_ref, mypan_ref, part_ref, got_ref, stat_ref, stats_ref,
-    vec_ref, yvec_ref, edges_ref, tail_ref, ends_ref, sums_ref, coef_ref,
+    vec_ref, yvec_ref, edges_ref, tail_ref, ends_ref, sums_ref, coef_ref, relay_ref,
     load_sem, first_sem, pan_send, pan_sem, stat_send, stat_sem,
     part_send, part_sem, v_send, v_sem, y_send, y_sem,
     edge_send, edge_sem, tail_send, tail_sem, sum_send, sum_sem,
+    head_send, relay_sem, kid_send, go_sem,
 ):
     rows_local, cols_local = a_hbm.shape
     tiles = cols_local // LANES
@@ -32,6 +35,17 @@
     slot = col - owner * split
     home = owner == row
     last = NB - 1
+    rows_y, rows_z = nrow // CORES, ncol // CHIPS_X
+    y, z = row // CORES, col // CHIPS_X
+    core, x = row - y * CORES, col - z * CHIPS_X
+    edge = rows_y - 1
+    source = col == 0
+    stand_in = col == 1
+    near = z < rows_z // 2
+    relay = near & (col > 0) & (y < edge)
+    kid_col = (rows_z - 1 - z) * CHIPS_X + x
+    near_y = y < rows_z // 2
+    corner = (y == edge) & (core == 0)
 
     def wrap(value, bound):
         return jnp.where(value >= bound, value - bound, value)
@@ -60,15 +74,41 @@
             device_id_type=pl.DeviceIdType.MESH,
         )
 
-    for dc in far_first(ncol)[:-1]:
-        greet(owner, wrap(col + dc, ncol))
+    @pl.when(jnp.logical_not(near))
+    def _():
+        via_x = jnp.where((z == rows_z - 1) & (x == 0), 1, x)
+        via_y = jnp.where(y == edge, 0, y)
+        greet(via_y * CORES + core, (rows_z - 1 - z) * CHIPS_X + via_x)
+
+    @pl.when(near & jnp.logical_not(home & source))
+    def _():
+        greet(owner, 0)
+
+    @pl.when(relay)
+    def _():
+        greet(kid_col // split, 0)
+
+    def greet_for(to_row, dc):
+        to_col = wrap(col + dc, ncol)
+        greet(to_row, jnp.where(to_col == 0, 1, to_col))
+
+    for dc in range(1, ncol - 1):
+        greet_for(owner, dc)
+
+    @pl.when(jnp.logical_not(stand_in & home))
+    def _():
+        greet_for(owner, ncol - 1)
 
     @pl.when(jnp.logical_not(home))
     def _():
-        greet(owner, col)
-
-    for dc in far_first(ncol)[:-1]:
-        greet(row, wrap(col + dc, ncol))
+        greet_for(owner, 0)
+
+    for dc in range(1, ncol - 1):
+        greet_for(row, dc)
+
+    @pl.when(jnp.logical_not(stand_in))
+    def _():
+        greet_for(row, ncol - 1)
 
     def send(src, dst, send_sem, recv_sem, to_row, to_col):
         pltpu.make_async_remote_copy(
@@ -125,8 +165,21 @@
 
             lax.fori_loop(0, tiles, turn, 0)
 
-    partners = split * nrow + ncol - 1
-    pl.semaphore_wait(barrier, jnp.where(home, partners - 1, partners))
+    one = jnp.where(home, 1, 0)
+    partners = split * nrow + ncol - 1 - one
+    kids = jnp.where(stand_in, 2, 1) * jnp.where(y == 0, 2, 1)
+    proxied = jnp.where(stand_in, split * nrow + ncol - 2 - 2 * one, 0)
+    others = partners + proxied + jnp.where(relay, kids, 0)
+    via = (nrow - CORES) * jnp.where(corner, 1, split)
+    first = jnp.where(near_y, split * nrow - one, via)
+    pl.semaphore_wait(barrier, jnp.where(source, first, others))
+
+    @pl.when(stand_in)
+    def _():
+        pl.semaphore_signal(
+            go_sem, inc=1, device_id=(row, col - 1),
+            device_id_type=pl.DeviceIdType.MESH,
+        )
 
     def pan_span(i):
         return pl.ds(0, 1) if i == 0 else pl.ds(2 * i - 1, 2)
@@ -141,7 +194,59 @@
                         pan_send, pan_sem.at[i],
                     )
 
-    send_pan(0)
+    head_span = pl.ds(0, 1)
+
+    @pl.when(source & near_y)
+    def _():
+        for spread in (spread_out, spread_here):
+            for h in range(split):
+                spread(
+                    h, pan_ref.at[head_span, h], mypan_ref.at[head_span],
+                    head_send, pan_sem.at[0],
+                )
+
+    @pl.when(source & jnp.logical_not(near_y))
+    def _():
+        for to_row in range(nrow - CORES):
+            for h in range(split):
+                to_x = core * split + h
+                moved = jnp.where((y == edge) & (to_x == 0), 1, 0)
+                send(
+                    pan_ref.at[head_span, h], relay_ref.at[pl.ds(moved, 1)],
+                    head_send, relay_sem,
+                    to_row, (rows_z - 1 - y) * CHIPS_X + to_x + moved,
+                )
+
+    def hand_on(act):
+        for i in range(2):
+            @pl.when(relay if i == 0 else relay & stand_in)
+            def _():
+                act(2 * i, row, kid_col - i)
+
+                @pl.when(y == 0)
+                def _():
+                    act(2 * i + 1, edge * CORES + core, kid_col - i)
+
+    def hand(i, to_row, to_col):
+        send(
+            relay_ref.at[pl.ds(i // 2, 1)], mypan_ref.at[head_span],
+            kid_send.at[i], pan_sem.at[0], to_row, to_col,
+        )
+
+    @pl.when(relay & stand_in)
+    def _():
+        expect(relay_ref, relay_sem)
+
+    @pl.when(relay & jnp.logical_not(stand_in))
+    def _():
+        expect(relay_ref.at[head_span], relay_sem)
+
+    hand_on(hand)
+
+    @pl.when(source)
+    def _():
+        pl.semaphore_wait(go_sem, 1)
+
     send_pan(1)
 
     def fold(acc, h, t, j):
@@ -375,9 +480,19 @@
     def _():
         expect(got_ref.at[pl.ds(0, NB + 1), pl.ds(0, ncol - 1)], edge_send)
 
-    @pl.when(col == 0)
-    def _():
-        settle(got_ref.at[pl.ds(0, NB + 1)], pan_send, row == 0)
+    hand_on(lambda i, to_row, to_col: expect(relay_ref.at[head_span], kid_send.at[i]))
+
+    @pl.when(source)
+    def _():
+        settle(got_ref.at[pl.ds(0, NB)], pan_send, row == 0)
+
+    @pl.when(source & near_y)
+    def _():
+        settle(got_ref.at[pl.ds(0, 1)], head_send, row == 0)
+
+    @pl.when(source & jnp.logical_not(near_y))
+    def _():
+        expect(got_ref.at[0, pl.ds(0, split * (nrow - CORES))], head_send)
 
     for k in range(NB):
         lay_out(refl_ref, refl_out, k)
@@ -439,6 +554,7 @@
             pltpu.VMEM((split, 2, tiles, LANES), F32),
             pltpu.VMEM((ncol, split, tiles, LANES), F32),
             pltpu.VMEM((3, tiles, LANES), F32),
+            pltpu.VMEM((2, tiles, LANES), F32),
             dma((blocks,)),
             dma(()),
             dma(()),
@@ -457,6 +573,10 @@
             dma(()),
             dma(()),
             dma(()),
+            dma(()),
+            dma(()),
+            dma((4,)),
+            pltpu.SemaphoreType.REGULAR,
         ],
         compiler_params=pltpu.CompilerParams(
             collective_id=0, has_side_effects=True, vmem_limit_bytes=56 * 2**20

time: 89.2 us -> 88.9 us (level)
  no operation moved by 1% of the time
where the time goes in v4:
time: 88.9 us; the launch traced here: 88.8 us
  Pallas kernels  88.1 us (99%)
    pallas_call x1, Pallas kernels, shards(): pl.pallas_call(functools.partial(kernel, nrow, ncol), out_shape=(panel, p...  87.5 us

profile of v4, /device:TPU:1, one launch (start us, length us, event | category | flops | bytes accessed | tf_op | source)
XLA Modules:
  0.0 88.8 jit_solution(1708314634729637469)
XLA Ops:
  0.6 87.5 %shard_map.46 = (f32[8,1024]{1,0:T(8,128)S(1)}, f32[8,1024]{1,0:T(8,128)S(1)}, f32[8,1024]{1,0:T(8,128)S(1)}, f32[8,8]{1,0:T(8,128)S(1)}) custom-call(f32[1024,512]{1,0:T(8,128)} %a_hbm.1), custom_call_target="tpu_custom_call" | custom-call | tf_op jit(solution)/shard_map/pallas_call | solution.py:534
  88.1 0.7 shard_map.47

commit v5 on v3

--- a/solution.py
+++ b/solution.py
@@ -12,16 +12,19 @@
 SUB = 8
 STATS = 16
 BLOCK = 256
+CORES = 2
+CHIPS_X = 4
 F32 = jnp.float32
 
 
 def kernel(
     nrow, ncol, a_hbm, hess_out, refl_out, wy_out, fac_ref,
     refl_ref, wy_ref, a_ref, first_ref, pan_ref, mypan_ref, part_ref, got_ref, stat_ref, stats_ref,
-    vec_ref, yvec_ref, edges_ref, tail_ref, ends_ref, sums_ref, coef_ref,
+    vec_ref, yvec_ref, edges_ref, tail_ref, ends_ref, sums_ref, coef_ref, relay_ref,
     load_sem, first_sem, pan_send, pan_sem, stat_send, stat_sem,
     part_send, part_sem, v_send, v_sem, y_send, y_sem,
     edge_send, edge_sem, tail_send, tail_sem, sum_send, sum_sem,
+    head_send, relay_sem, kid_send, go_sem,
 ):
     rows_local, cols_local = a_hbm.shape
     tiles = cols_local // LANES
@@ -32,6 +35,14 @@
     slot = col - owner * split
     home = owner == row
     last = NB - 1
+    planes = ncol // CHIPS_X
+    y, z = row // CORES, col // CHIPS_X
+    core, x = row - y * CORES, col - z * CHIPS_X
+    front = z == 0
+    source = col == 0
+    relay = front & (col > 0)
+    stand_in = z == 1
+    twice = col == 1
 
     def wrap(value, bound):
         return jnp.where(value >= bound, value - bound, value)
@@ -60,15 +71,36 @@
             device_id_type=pl.DeviceIdType.MESH,
         )
 
-    for dc in far_first(ncol)[:-1]:
-        greet(owner, wrap(col + dc, ncol))
+    @pl.when(jnp.logical_not(front))
+    def _():
+        greet(row, jnp.where(x == 0, 1, x))
+
+    @pl.when(front & jnp.logical_not(home & source))
+    def _():
+        greet(owner, 0)
+
+    @pl.when(relay)
+    def _():
+        for plane in range(1, planes):
+            greet(plane * CORES + owner, 0)
+
+    def greet_for(to_row, dc):
+        to_col = wrap(col + dc, ncol)
+        greet(to_row, jnp.where(to_col < CHIPS_X, to_col + CHIPS_X, to_col))
+
+    behind = ncol - CHIPS_X
+    for to_row, skip in ((owner, stand_in & home), (row, stand_in)):
+        for dc in range(1, ncol):
+            if dc != behind:
+                greet_for(to_row, dc)
+
+        @pl.when(jnp.logical_not(skip))
+        def _():
+            greet_for(to_row, behind)
 
     @pl.when(jnp.logical_not(home))
     def _():
-        greet(owner, col)
-
-    for dc in far_first(ncol)[:-1]:
-        greet(row, wrap(col + dc, ncol))
+        greet_for(owner, 0)
 
     def send(src, dst, send_sem, recv_sem, to_row, to_col):
         pltpu.make_async_remote_copy(
@@ -125,8 +157,23 @@
 
             lax.fori_loop(0, tiles, turn, 0)
 
-    partners = split * nrow + ncol - 1
-    pl.semaphore_wait(barrier, jnp.where(home, partners - 1, partners))
+    one = jnp.where(home, 1, 0)
+    partners = split * nrow + ncol - 1 - one
+    front_home = jnp.where((col - CHIPS_X) // split == row, 1, 0)
+    proxied = partners - 1 + one - front_home - one
+    kids = (planes - 1) * jnp.where(twice, 2, 1)
+    first = jnp.where(core == 0, nrow, split * nrow)
+    first = jnp.where(y == 0, split * nrow - one, first)
+    count = jnp.where(stand_in, partners + proxied, partners)
+    count = jnp.where(source, first, jnp.where(relay, kids, count))
+    pl.semaphore_wait(barrier, count)
+
+    @pl.when(stand_in)
+    def _():
+        pl.semaphore_signal(
+            go_sem, inc=1, device_id=(row, col - CHIPS_X),
+            device_id_type=pl.DeviceIdType.MESH,
+        )
 
     def pan_span(i):
         return pl.ds(0, 1) if i == 0 else pl.ds(2 * i - 1, 2)
@@ -141,7 +188,49 @@
                         pan_send, pan_sem.at[i],
                     )
 
-    send_pan(0)
+    head_span = pl.ds(0, 1)
+
+    @pl.when(source & (y == 0))
+    def _():
+        for spread in (spread_out, spread_here):
+            for h in range(split):
+                spread(
+                    h, pan_ref.at[head_span, h], mypan_ref.at[head_span],
+                    head_send, pan_sem.at[0],
+                )
+
+    @pl.when(source & (y > 0))
+    def _():
+        for dr in far_first(nrow):
+            for h in range(split):
+                to_x = core * split + h
+                moved = jnp.where(to_x == 0, 1, 0)
+                send(
+                    pan_ref.at[head_span, h], relay_ref.at[moved, pl.ds(y, 1)],
+                    head_send, relay_sem.at[moved, y], wrap(row + dr, nrow), to_x + moved,
+                )
+
+    def hand_on(i):
+        for plane in far_first(planes)[:-1]:
+            piece = relay_ref.at[i, pl.ds(plane, 1)]
+            expect(piece, relay_sem.at[i, plane])
+            send(
+                piece, mypan_ref.at[head_span], kid_send.at[i], pan_sem.at[0],
+                row, plane * CHIPS_X + x - i,
+            )
+
+    @pl.when(relay)
+    def _():
+        hand_on(0)
+
+    @pl.when(twice)
+    def _():
+        hand_on(1)
+
+    @pl.when(front)
+    def _():
+        pl.semaphore_wait(go_sem, 1)
+
     send_pan(1)
 
     def fold(acc, h, t, j):
@@ -375,9 +464,15 @@
     def _():
         expect(got_ref.at[pl.ds(0, NB + 1), pl.ds(0, ncol - 1)], edge_send)
 
-    @pl.when(col == 0)
-    def _():
-        settle(got_ref.at[pl.ds(0, NB + 1)], pan_send, row == 0)
+    for i, sent in enumerate((relay, twice)):
+        @pl.when(sent)
+        def _():
+            expect(relay_ref.at[i, pl.ds(1, planes - 1)], kid_send.at[i])
+
+    @pl.when(source)
+    def _():
+        settle(got_ref.at[pl.ds(0, NB)], pan_send, row == 0)
+        settle(got_ref.at[pl.ds(0, 1)], head_send, row == 0)
 
     for k in range(NB):
         lay_out(refl_ref, refl_out, k)
@@ -439,6 +534,7 @@
             pltpu.VMEM((split, 2, tiles, LANES), F32),
             pltpu.VMEM((ncol, split, tiles, LANES), F32),
             pltpu.VMEM((3, tiles, LANES), F32),
+            pltpu.VMEM((2, ncol // CHIPS_X, tiles, LANES), F32),
             dma((blocks,)),
             dma(()),
             dma(()),
@@ -457,6 +553,10 @@
             dma(()),
             dma(()),
             dma(()),
+            dma(()),
+            dma((2, ncol // CHIPS_X)),
+            dma((2,)),
+            pltpu.SemaphoreType.REGULAR,
         ],
         compiler_params=pltpu.CompilerParams(
             collective_id=0, has_side_effects=True, vmem_limit_bytes=56 * 2**20

time: 89.2 us -> 86.1 us (0.965)
  Pallas kernels: 88.2 us -> 85.4 us
    pallas_call x1, Pallas kernels: 87.5 us -> 84.7 us  [shards(): pl.pallas_call(functools.partial(kernel, nrow, ncol), out_shape=(panel, p...]
where the time goes in v5:
time: 86.1 us; the launch traced here: 86 us
  Pallas kernels  85.4 us (99%)
    pallas_call x1, Pallas kernels, shards(): pl.pallas_call(functools.partial(kernel, nrow, ncol), out_shape=(panel, p...  84.7 us

profile of v5, /device:TPU:1, one launch (start us, length us, event | category | flops | bytes accessed | tf_op | source)
XLA Modules:
  0.0 86.0 jit_solution(7205007631485401424)
XLA Ops:
  0.6 84.7 %shard_map.46 = (f32[8,1024]{1,0:T(8,128)S(1)}, f32[8,1024]{1,0:T(8,128)S(1)}, f32[8,1024]{1,0:T(8,128)S(1)}, f32[8,8]{1,0:T(8,128)S(1)}) custom-call(f32[1024,512]{1,0:T(8,128)} %a_hbm.1), custom_call_target="tpu_custom_call" | custom-call | tf_op jit(solution)/shard_map/pallas_call | solution.py:514
  85.3 0.7 shard_map.47

commit v6 on v5

--- a/solution.py
+++ b/solution.py
@@ -176,7 +176,7 @@
         )
 
     def pan_span(i):
-        return pl.ds(0, 1) if i == 0 else pl.ds(2 * i - 1, 2)
+        return pl.ds(2 * i, min(2, NB + 1 - 2 * i))
 
     def send_pan(i):
         @pl.when(col == 0)
@@ -188,7 +188,7 @@
                         pan_send, pan_sem.at[i],
                     )
 
-    head_span = pl.ds(0, 1)
+    head_span = pan_span(0)
 
     @pl.when(source & (y == 0))
     def _():
@@ -206,13 +206,13 @@
                 to_x = core * split + h
                 moved = jnp.where(to_x == 0, 1, 0)
                 send(
-                    pan_ref.at[head_span, h], relay_ref.at[moved, pl.ds(y, 1)],
+                    pan_ref.at[head_span, h], relay_ref.at[moved, y],
                     head_send, relay_sem.at[moved, y], wrap(row + dr, nrow), to_x + moved,
                 )
 
     def hand_on(i):
         for plane in far_first(planes)[:-1]:
-            piece = relay_ref.at[i, pl.ds(plane, 1)]
+            piece = relay_ref.at[i, plane]
             expect(piece, relay_sem.at[i, plane])
             send(
                 piece, mypan_ref.at[head_span], kid_send.at[i], pan_sem.at[0],
@@ -230,8 +230,6 @@
     @pl.when(front)
     def _():
         pl.semaphore_wait(go_sem, 1)
-
-    send_pan(1)
 
     def fold(acc, h, t, j):
         part_ref[j, h, t : t + 1, :] = jnp.sum(acc.T, axis=0, keepdims=True)
@@ -322,7 +320,7 @@
             send_stats(j, b)
             if j > 0:
                 publish(yvec_ref.at[j - 1], wy_ref, j - 1, y_send, y_sem)
-            if 0 < j < NB // 2:
+            if j < NB // 2:
                 send_pan(j + 1)
         else:
             send_stats(j, b)
@@ -382,9 +380,8 @@
         tops.append(vtop)
         hrow = jnp.where(lane == j + 1, -signed, above)
         hess_out[j : j + 1, 0:LANES] = jnp.where(row == 0, hrow, F32(0.0))
-        if j == 0 or 1 < j <= NB // 2:
-            i = max(j, 1)
-            expect(mypan_ref.at[pan_span(i)], pan_sem.at[i])
+        if 0 < j <= NB // 2:
+            expect(mypan_ref.at[pan_span(j)], pan_sem.at[j])
         if j < last:
             drop = jnp.zeros((tiles, LANES), F32)
             for k in range(j):
@@ -471,8 +468,8 @@
 
     @pl.when(source)
     def _():
-        settle(got_ref.at[pl.ds(0, NB)], pan_send, row == 0)
-        settle(got_ref.at[pl.ds(0, 1)], head_send, row == 0)
+        settle(got_ref.at[pl.ds(0, NB - 1)], pan_send, row == 0)
+        settle(got_ref.at[pl.ds(0, 2)], head_send, row == 0)
 
     for k in range(NB):
         lay_out(refl_ref, refl_out, k)
@@ -534,7 +531,7 @@
             pltpu.VMEM((split, 2, tiles, LANES), F32),
             pltpu.VMEM((ncol, split, tiles, LANES), F32),
             pltpu.VMEM((3, tiles, LANES), F32),
-            pltpu.VMEM((2, ncol // CHIPS_X, tiles, LANES), F32),
+            pltpu.VMEM((2, ncol // CHIPS_X, 2, tiles, LANES), F32),
             dma((blocks,)),
             dma(()),
             dma(()),

time: 86.1 us -> 84.5 us (0.981)
  Pallas kernels: 85.4 us -> 83.8 us
    pallas_call x1, Pallas kernels: 84.7 us -> 83.1 us  [shards(): pl.pallas_call(functools.partial(kernel, nrow, ncol), out_shape=(panel, p...]
where the time goes in v6:
time: 84.5 us; the launch traced here: 84.4 us
  Pallas kernels  83.8 us (99%)
    pallas_call x1, Pallas kernels, shards(): pl.pallas_call(functools.partial(kernel, nrow, ncol), out_shape=(panel, p...  83.1 us

profile of v6, /device:TPU:1, one launch (start us, length us, event | category | flops | bytes accessed | tf_op | source)
XLA Modules:
  0.0 84.4 jit_solution(7717972147726470645)
XLA Ops:
  0.6 83.1 %shard_map.46 = (f32[8,1024]{1,0:T(8,128)S(1)}, f32[8,1024]{1,0:T(8,128)S(1)}, f32[8,1024]{1,0:T(8,128)S(1)}, f32[8,8]{1,0:T(8,128)S(1)}) custom-call(f32[1024,512]{1,0:T(8,128)} %a_hbm.1), custom_call_target="tpu_custom_call" | custom-call | tf_op jit(solution)/shard_map/pallas_call | solution.py:511
  83.7 0.7 shard_map.47

commit v7 on v6

--- a/solution.py
+++ b/solution.py
@@ -227,10 +227,6 @@
     def _():
         hand_on(1)
 
-    @pl.when(front)
-    def _():
-        pl.semaphore_wait(go_sem, 1)
-
     def fold(acc, h, t, j):
         part_ref[j, h, t : t + 1, :] = jnp.sum(acc.T, axis=0, keepdims=True)
 
@@ -310,6 +306,11 @@
     for j in range(NB):
         if j < last:
             def share(spread, h):
+                if j == 0 and h == 0 and spread is spread_out:
+                    @pl.when(front)
+                    def _():
+                        pl.semaphore_wait(go_sem, 1)
+
                 spread(
                     h, part_ref.at[j, h], got_ref.at[j, col], part_send, part_sem.at[j]
                 )
@@ -323,10 +324,9 @@
             if j < NB // 2:
                 send_pan(j + 1)
         else:
-            send_stats(j, b)
             tail_ref[0] = b
             tail_ref[1] = yvec_ref[j - 1]
-            matvec(j, b, lambda h: None)
+            matvec(j, b, lambda h: send_stats(j, b) if h == 0 else None)
             sums_ref[col] = part_ref[j]
             to_peers(part_ref.at[j], sums_ref.at[col], sum_send, sum_sem)
             own_rows(tail_ref, lambda at: ends_ref.at[at], tail_send, tail_sem)

time: 84.5 us -> 85 us (level)
  no operation moved by 1% of the time
where the time goes in v7:
time: 85 us; the launch traced here: 84.9 us
  Pallas kernels  84.2 us (99%)
    pallas_call x1, Pallas kernels, shards(): pl.pallas_call(functools.partial(kernel, nrow, ncol), out_shape=(panel, p...  83.6 us

profile of v7, /device:TPU:1, one launch (start us, length us, event | category | flops | bytes accessed | tf_op | source)
XLA Modules:
  0.0 84.9 jit_solution(527752141812670088)
XLA Ops:
  0.6 83.6 %shard_map.46 = (f32[8,1024]{1,0:T(8,128)S(1)}, f32[8,1024]{1,0:T(8,128)S(1)}, f32[8,1024]{1,0:T(8,128)S(1)}, f32[8,8]{1,0:T(8,128)S(1)}) custom-call(f32[1024,512]{1,0:T(8,128)} %a_hbm.1), custom_call_target="tpu_custom_call" | custom-call | tf_op jit(solution)/shard_map/pallas_call | solution.py:511
  84.2 0.7 shard_map.47
